TPU v7x, 32 devices: a whole 2x2x4 slice. The times are simulated.
32 devices in a mesh: sample: 2 (over x), sy: 4 (over y, core), sz: 4 (over z).
Axes of the slice: x: 2, y: 2, z: 4, core: 2. Of those that a mesh axis runs over, the one named last changes fastest.
Arguments:
- volume: bfloat16 [2, 32, 16, 32, 128], P('sample', None, 'sz', 'sy'), may hold values from -22.5 to 22.5
- amax_history: float32 [4, 16], replicated, may hold values from 0.48 to 2.5
- conv_first: bfloat16 [27, 32, 32], replicated, may hold values from -0.21875 to 0.21875
- conv_second: bfloat16 [27, 32, 32], replicated, may hold values from -0.21875 to 0.21875
- conv_third: bfloat16 [27, 64, 32], P(None, 'sy'), may hold values from -0.21875 to 0.21875
- conv_fourth: bfloat16 [27, 64, 64], P(None, 'sy'), may hold values from -0.15625 to 0.15625
- gain_fine: float32 [2, 32], replicated, may hold values from 0.5 to 1.5
- shift_fine: float32 [2, 32], replicated, may hold values from -0.5 to 0.5
- gain_coarse: float32 [2, 64], P(None, 'sy'), may hold values from 0.5 to 1.5
- shift_coarse: float32 [2, 64], P(None, 'sy'), may hold values from -0.5 to 0.5
Outputs:
- skip_features: bfloat16 [2, 32, 16, 32, 128], P('sample', None, 'sz', 'sy')
- coarse_features: bfloat16 [2, 64, 8, 1024], P('sample', 'sy', 'sz')
- amax_now: float32 [4], replicated
All inputs are finite; a program needn't handle non-finite values.
Results may differ from a plain program's by a relative error of at most 0.012.
Values may be sent and summed in bfloat16 or wider, within the bound.
No kernel may reach another device: no remote copies, remote signals or barrier semaphores. Data moves between devices by JAX's collectives and lax.ppermute only.
A program may use at most 128 MiB of HBM per device.

v0:
```python
import jax
import jax.numpy as jnp
from jax import lax
from jax.sharding import PartitionSpec as P

norm_eps = 1e-05
leak_slope = 0.01


def padded_2(cells, sides, width):
    for axis, dim in sides:
        count = lax.axis_size(axis)
        ends = count - 1
        head = lax.slice_in_dim(cells, 0, width, axis=dim)
        tail = lax.slice_in_dim(cells, cells.shape[dim] - width, cells.shape[dim], axis=dim)
        cells = jnp.concatenate(
            [
                lax.ppermute(tail, axis, [(i, (i + 1) % count) for i in range(ends)]),
                cells,
                lax.ppermute(head, axis, [((i + 1) % count, i) for i in range(ends)]),
            ],
            axis=dim,
        )
    return cells


def limited(values, bound):
    return jnp.clip(values.astype(jnp.float32), -bound, bound).astype(jnp.bfloat16)


def fine_faces(values):
    return padded_2(values, (("sy", 2), ("sz", 1)), 1)


def coarse_faces(values):
    return padded_2(values, (("sz", 1),), 1)


def fine_stats(values):
    flat_rows = values.reshape(values.shape[0], -1)
    return lax.psum(
        (jnp.sum(flat_rows, axis=1), jnp.sum(flat_rows * flat_rows, axis=1)), ("sy", "sz")
    )


def coarse_stats(values):
    flat_rows = values.reshape(values.shape[0], -1)
    return lax.psum((jnp.sum(flat_rows, axis=1), jnp.sum(flat_rows * flat_rows, axis=1)), "sz")


def apply_norm(values, moments, cell_count, gains, offset):
    chan_mean = moments[0] / cell_count
    spread = moments[1] / cell_count - chan_mean * chan_mean
    scaling = lax.rsqrt(spread + norm_eps) * gains
    shaped = (-1,) + (1,) * (values.ndim - 1)
    normed = (values - chan_mean.reshape(shaped)) * scaling.reshape(shaped) + offset.reshape(shaped)
    return jnp.where(normed >= 0, normed, leak_slope * normed).astype(jnp.bfloat16)


def level_one_conv(padded, weight):
    channels, depth_cells, height_cells, width_cells = padded.shape
    out_depth = depth_cells - 2
    out_height = height_cells - 2
    out_chan = weight.shape[1]
    widened = jnp.pad(padded, ((0, 0), (0, 0), (0, 0), (1, 1)))
    stacked = jnp.concatenate(
        [widened[:, :, :, x_tap : x_tap + width_cells] for x_tap in range(3)], axis=0
    )
    summed = jnp.zeros((out_chan, out_depth * out_height * width_cells), jnp.float32)
    for z_tap in range(3):
        for y_tap in range(3):
            first_tap = z_tap * 9 + y_tap * 3
            taps = weight[first_tap : first_tap + 3]
            matrix = jnp.transpose(taps, (1, 0, 2)).reshape(out_chan, 3 * channels)
            window = stacked[:, z_tap : z_tap + out_depth, y_tap : y_tap + out_height, :].reshape(
                3 * channels, -1
            )
            summed = summed + jnp.dot(matrix, window, preferred_element_type=jnp.float32)
    return summed.reshape(out_chan, out_depth, out_height, width_cells)


def level_two_conv(padded, weight, row_len):
    channels, depth_cells, flat_len = padded.shape
    out_depth = depth_cells - 2
    out_chan = weight.shape[1]
    column = lax.broadcasted_iota(jnp.int32, (1, 1, flat_len), 2) % row_len
    blank = jnp.zeros((), padded.dtype)
    sources = (
        jnp.where(column == row_len - 1, blank, padded),
        padded,
        jnp.where(column == 0, blank, padded),
    )
    wide_len = flat_len + 2 * row_len
    stacked = jnp.concatenate(
        [
            jnp.pad(sources[x_tap], ((0, 0), (0, 0), (row_len + 1, row_len + 1)))[
                :, :, x_tap : x_tap + wide_len
            ]
            for x_tap in range(3)
        ],
        axis=0,
    )
    summed = jnp.zeros((out_chan, out_depth * flat_len), jnp.float32)
    for z_tap in range(3):
        for y_tap in range(3):
            first_tap = z_tap * 9 + y_tap * 3
            taps = weight[first_tap : first_tap + 3]
            matrix = jnp.transpose(taps, (1, 0, 2)).reshape(out_chan, 3 * channels)
            window = stacked[
                :, z_tap : z_tap + out_depth, y_tap * row_len : y_tap * row_len + flat_len
            ].reshape(3 * channels, -1)
            summed = summed + jnp.dot(matrix, window, preferred_element_type=jnp.float32)
    return summed.reshape(out_chan, out_depth, flat_len)


def magnitude(values):
    return jnp.max(jnp.abs(values.astype(jnp.float32)))


def per_device(
    volume,
    amax_history,
    conv_first,
    conv_second,
    conv_third,
    conv_fourth,
    gain_fine,
    shift_fine,
    gain_coarse,
    shift_coarse,
):
    bounds = jnp.max(amax_history, axis=1)
    sample_count, channels, z_cells, y_cells, x_cells = volume.shape
    z_groups = lax.axis_size("sz")
    y_groups = lax.axis_size("sy")
    half_x = x_cells // 2
    half_z = z_cells // 2
    fine_cells = float(z_cells * z_groups * y_cells * y_groups * x_cells)
    coarse_cells = float(half_z * z_groups * (y_cells // 2) * y_groups * half_x)
    source = volume[0]
    layer_peaks = [magnitude(source)]
    first_in = limited(source, bounds[0])
    first_out = level_one_conv(fine_faces(first_in), conv_first)
    hidden = apply_norm(first_out, fine_stats(first_out), fine_cells, gain_fine[0], shift_fine[0])
    layer_peaks.append(magnitude(hidden))
    second_out = level_one_conv(fine_faces(limited(hidden, bounds[1])), conv_second)
    skip_out = apply_norm(
        second_out, fine_stats(second_out), fine_cells, gain_fine[1], shift_fine[1]
    )
    skip_list = [skip_out]
    blocks = skip_out.reshape(channels, half_z, 2, y_cells // 2, 2, half_x, 2)
    pooled = jnp.max(blocks, axis=(2, 4, 6))
    layer_peaks.append(magnitude(pooled))
    gathered = lax.all_gather(limited(pooled, bounds[2]), "sy", axis=2, tiled=True)
    flat_in = gathered.reshape(channels, half_z, -1)
    third_out = level_two_conv(coarse_faces(flat_in), conv_third, half_x)
    coarse_hidden = apply_norm(
        third_out, coarse_stats(third_out), coarse_cells, gain_coarse[0], shift_coarse[0]
    )
    layer_peaks.append(magnitude(coarse_hidden))
    edged = coarse_faces(limited(coarse_hidden, bounds[3]))
    fourth_out = level_two_conv(
        lax.all_gather(edged, "sy", axis=0, tiled=True), conv_fourth, half_x
    )
    coarse_list = [
        apply_norm(
            fourth_out, coarse_stats(fourth_out), coarse_cells, gain_coarse[1], shift_coarse[1]
        )
    ]
    peak_rows = [jnp.stack(layer_peaks)]
    peaks = jnp.max(jnp.stack(peak_rows), axis=0)
    peaks = lax.pmax(peaks, ("sample", "sy", "sz"))
    return (jnp.stack(skip_list), jnp.stack(coarse_list), peaks)


def solution(mesh):
    return jax.shard_map(
        per_device,
        mesh=mesh,
        in_specs=(
            P("sample", None, "sz", "sy", None),
            P(),
            P(),
            P(),
            P(None, "sy", None),
            P(None, "sy", None),
            P(),
            P(),
            P(None, "sy"),
            P(None, "sy"),
        ),
        out_specs=(P("sample", None, "sz", "sy", None), P("sample", "sy", "sz", None), P()),
        check_vma=False,
    )
```

profile of v0, /device:TPU:0, one launch (start us, length us, event | category | flops | bytes accessed | tf_op | source)
XLA Modules:
  0.0 249.3 jit_solution(14499063451682183801)
XLA Ops:
  2.7 1.7 fusion.64
  4.5 2.4 collective-permute-start
  13.2 1.7 fusion.57
  16.6 4.3 %collective-permute-start.2 = (bf16[32,1,10,128]{3,2,1,0:T(8,128)(2,1)S(1)}, bf16[32,1,10,128]{3,2,1,0:T(8,128)(2,1)S(1)}, u32[]{:S(2)}, u32[]{:S(2)}) collective-permute-start(bf16[32,1,10,128]{3,2,1,0:T(8,128)(2,1)S(1)} %get-tuple-element.55), channel_id=1, source_target_pairs={{0,1},{1,2},{2,3},{4,5},{5,6},{6,7},{8,9},{9,10},{10,11},{12,13},{... | collective-permute-start | bytes 245768 | tf_op jit(solution)/shard_map/ppermute | solution.py:18
  23.4 4.6 %collective-permute-done.3 = bf16[32,1,10,128]{3,2,1,0:T(8,128)(2,1)S(1)} collective-permute-done((bf16[32,1,10,128]{3,2,1,0:T(8,128)(2,1)S(1)}, bf16[32,1,10,128]{3,2,1,0:T(8,128)(2,1)S(1)}, u32[]{:S(2)}, u32[]{:S(2)}) %collective-permute-start.3) | collective-permute-done | bytes 81952 | tf_op jit(solution)/shard_map/ppermute | solution.py:20
  28.0 1.8 fusion.11
  31.4 1.5 fusion.77
  37.0 31.8 %all-reduce.9 = (f32[32]{0:T(128)S(1)}, f32[32]{0:T(128)S(1)}) all-reduce(f32[32]{0:T(128)S(1)} %get-tuple-element.119, f32[32]{0:T(128)S(1)} %reduce_sum.72), channel_id=1, replica_groups=mesh['sample'=2,'sy'=4,'sz'=4] {'sy','sz'}, use_global_device_ids=true, to_apply=%region_4.5 | all-reduce | flops 64 | bytes 512 | tf_op jit(solution)/shard_map/psum | solution.py:41
  77.8 2.6 %collective-permute-start.6 = (bf16[32,1,10,128]{3,2,1,0:T(8,128)(2,1)S(1)}, bf16[32,1,10,128]{3,2,1,0:T(8,128)(2,1)S(1)}, u32[]{:S(2)}, u32[]{:S(2)}) collective-permute-start(bf16[32,1,10,128]{3,2,1,0:T(8,128)(2,1)S(1)} %get-tuple-element.53), channel_id=1, source_target_pairs={{0,1},{1,2},{2,3},{4,5},{5,6},{6,7},{8,9},{9,10},{10,11},{12,13},{... | collective-permute-start | bytes 245768 | tf_op jit(solution)/shard_map/ppermute | solution.py:18
  82.9 4.4 %collective-permute-done.7 = bf16[32,1,10,128]{3,2,1,0:T(8,128)(2,1)S(1)} collective-permute-done((bf16[32,1,10,128]{3,2,1,0:T(8,128)(2,1)S(1)}, bf16[32,1,10,128]{3,2,1,0:T(8,128)(2,1)S(1)}, u32[]{:S(2)}, u32[]{:S(2)}) %collective-permute-start.7) | collective-permute-done | bytes 81952 | tf_op jit(solution)/shard_map/ppermute | solution.py:20
  87.3 1.8 select_maximum_fusion
  90.7 1.5 fusion.76
  96.9 30.0 %all-reduce.8 = (f32[32]{0:T(128)S(1)}, f32[32]{0:T(128)S(1)}) all-reduce(f32[32]{0:T(128)S(1)} %get-tuple-element.121, f32[32]{0:T(128)S(1)} %reduce_sum.74), channel_id=1, replica_groups=mesh['sample'=2,'sy'=4,'sz'=4] {'sy','sz'}, use_global_device_ids=true, to_apply=%region_8.9 | all-reduce | flops 64 | bytes 512 | tf_op jit(solution)/shard_map/psum | solution.py:41
  126.9 2.9 %fusion.16 = bf16[32,2,4,64]{0,3,2,1:T(8,128)(2,1)S(1)} fusion(f32[32]{0:T(128)S(1)} %get-tuple-element.105, f32[32]{0:T(128)S(1)} %get-tuple-element.116, f32[32,2,2,4,2,64,2]{0,6,5,4,3,2,1:T(2,128)S(1)} %bitcast.322, f32[32]{0:T(128)S(1)} %get-tuple-element.115), kind=kLoop, calls=%fused_computation.59 | loop fusion | flops 1032192 | bytes 557440 | tf_op jit(solution)/shard_map/reduce_max | solution.py:152
  130.7 8.9 %all_gather.6 = bf16[32,2,16,64]{3,0,1,2:T(8,128)(2,1)S(1)} all-gather(bf16[32,2,4,64]{3,0,1,2:T(8,128)(2,1)S(1)} %copy.195), channel_id=1, replica_groups=mesh['sample'=2,'sy'=4,'sz'=4] {'sy'}, dimensions={2}, use_global_device_ids=true | all-gather | bytes 163840 | tf_op jit(solution)/shard_map/all_gather | solution.py:154
  141.3 4.8 %collective-permute-start.8 = (bf16[32,1,1024]{2,0,1:T(8,128)(2,1)S(1)}, bf16[32,1,1024]{2,0,1:T(8,128)(2,1)S(1)}, u32[]{:S(2)}, u32[]{:S(2)}) collective-permute-start(bf16[32,1,1024]{2,0,1:T(8,128)(2,1)S(1)} %get-tuple-element.82), channel_id=1, source_target_pairs={{0,1},{1,2},{2,3},{4,5},{5,6},{6,7},{8,9},{9,10},{10,11},{12,13},{... | collective-permute-start | bytes 196616 | tf_op jit(solution)/shard_map/ppermute | solution.py:18
  151.5 11.7 %all-reduce.11 = (f32[16]{0:T(128)S(1)}, f32[16]{0:T(128)S(1)}) all-reduce(f32[16]{0:T(128)S(1)} %get-tuple-element.123, f32[16]{0:T(128)S(1)} %reduce_sum.76), channel_id=1, replica_groups=mesh['sample'=2,'sy'=4,'sz'=4] {'sz'}, use_global_device_ids=true, to_apply=%region_13.14 | all-reduce | flops 32 | bytes 256 | tf_op jit(solution)/shard_map/psum | solution.py:48
  164.9 2.0 collective-permute-start.10
  168.2 2.6 %pad_maximum_fusion.11 = f32[4]{0:T(128)S(1)} fusion(f32[1]{0:T(128)} %bitcast.57, f32[1]{0:T(128)} %bitcast.56, f32[1]{0:T(128)} %bitcast.55, f32[1]{0:T(128)} %bitcast.54), kind=kLoop, calls=%fused_computation.203 | loop fusion | flops 12 | bytes 32 | tf_op jit(solution)/shard_map/stack | solution.py:170
  171.8 41.5 %pmax.7 = f32[4]{0:T(128)} all-reduce(f32[4]{0:T(128)S(1)} %pad_maximum_fusion.11), channel_id=1, replica_groups=mesh['sample'=2,'sy'=4,'sz'=4] {'sample','sy','sz'}, use_global_device_ids=true, to_apply=%region_22.23 | all-reduce | flops 4 | bytes 32 | tf_op jit(solution)/shard_map/pmax | solution.py:172
  213.5 8.1 %all_gather.7 = bf16[64,4,1024]{2,1,0:T(4,128)(2,1)S(1)} all-gather(bf16[16,4,1024]{2,1,0:T(4,128)(2,1)S(1)} %pad_maximum_fusion.10), channel_id=1, replica_groups=mesh['sample'=2,'sy'=4,'sz'=4] {'sy'}, dimensions={0}, use_global_device_ids=true | all-gather | bytes 655360 | tf_op jit(solution)/shard_map/all_gather | solution.py:163
  223.3 3.0 %pad_maximum_fusion.2 = bf16[192,4,1152]{2,1,0:T(4,128)(2,1)S(1)} fusion(bf16[64,4,1152]{2,1,0:T(4,128)(2,1)S(1)} %pad_slice_fusion, bf16[64,4,1152]{2,1,0:T(4,128)(2,1)S(1)} %pad_slice_fusion.1, bf16[64,4,1152]{2,1,0:T(4,128)(2,1)S(1)} %pad_slice_fusion.2), kind=kLoop, calls=%fused_computation.39 | loop fusion | flops 1769472 | bytes 3538944 | tf_op jit(solution)/shard_map/concatenate | solution.py:94
  226.3 8.0 %fusion.78 = (bf16[192,2,1024]{2,1,0:T(2,128)(2,1)S(1)}, bf16[192,2,1024]{2,1,0:T(2,128)(2,1)S(1)}, bf16[192,2,1024]{2,1,0:T(2,128)(2,1)S(1)}, bf16[192,2,1024]{...) fusion(bf16[192,4,1152]{2,1,0:T(4,128)(2,1)S(1)} %pad_maximum_f, ...), kind=kLoop, calls=%fused_computation.218 | loop fusion | bytes 14155776 | tf_op jit(solution)/shard_map/slice | solution.py:109
  238.6 9.9 %all-reduce.10 = (f32[16]{0:T(128)S(1)}, f32[16]{0:T(128)S(1)}) all-reduce(f32[16]{0:T(128)S(1)} %get-tuple-element.125, f32[16]{0:T(128)S(1)} %reduce_sum.78), channel_id=1, replica_groups=mesh['sample'=2,'sy'=4,'sz'=4] {'sz'}, use_global_device_ids=true, to_apply=%region_17.18 | all-reduce | flops 32 | bytes 256 | tf_op jit(solution)/shard_map/psum | solution.py:48
  (205 shorter events, 51.8 us)
Async XLA Ops:
  4.5 12.0 %collective-permute-start = (bf16[32,4,1,128]{3,2,1,0:T(2,128)(2,1)S(1)}, bf16[32,4,1,128]{3,2,1,0:T(2,128)(2,1)S(1)}, u32[]{:S(2)}, u32[]{:S(2)}) collective-permute-start(bf16[32,4,1,128]{3,2,1,0:T(2,128)(2,1)S(1)} %get-tuple-element.61), channel_id=1, source_target_pairs={{0,4},{4,8},{8,12},{1,5},{5,9},{9,13},{2,6},{6,10},{10,14},{3,7},{... | collective-permute-start | bytes 98312 | tf_op jit(solution)/shard_map/ppermute | solution.py:18
  6.9 9.6 %collective-permute-start.1 = (bf16[32,4,1,128]{3,2,1,0:T(2,128)(2,1)S(1)}, bf16[32,4,1,128]{3,2,1,0:T(2,128)(2,1)S(1)}, u32[]{:S(2)}, u32[]{:S(2)}) collective-permute-start(bf16[32,4,1,128]{3,2,1,0:T(2,128)(2,1)S(1)} %get-tuple-element.62), channel_id=1, source_target_pairs={{4,0},{8,4},{12,8},{5,1},{9,5},{13,9},{6,2},{10,6},{14,10},{7,3},{... | collective-permute-start | bytes 98312 | tf_op jit(solution)/shard_map/ppermute | solution.py:20
  16.6 6.8 %collective-permute-start.2 = (bf16[32,1,10,128]{3,2,1,0:T(8,128)(2,1)S(1)}, bf16[32,1,10,128]{3,2,1,0:T(8,128)(2,1)S(1)}, u32[]{:S(2)}, u32[]{:S(2)}) collective-permute-start(bf16[32,1,10,128]{3,2,1,0:T(8,128)(2,1)S(1)} %get-tuple-element.55), channel_id=1, source_target_pairs={{0,1},{1,2},{2,3},{4,5},{5,6},{6,7},{8,9},{9,10},{10,11},{12,13},{... | collective-permute-start | bytes 245768 | tf_op jit(solution)/shard_map/ppermute | solution.py:18
  20.9 7.1 %collective-permute-start.3 = (bf16[32,1,10,128]{3,2,1,0:T(8,128)(2,1)S(1)}, bf16[32,1,10,128]{3,2,1,0:T(8,128)(2,1)S(1)}, u32[]{:S(2)}, u32[]{:S(2)}) collective-permute-start(bf16[32,1,10,128]{3,2,1,0:T(8,128)(2,1)S(1)} %get-tuple-element.56), channel_id=1, source_target_pairs={{1,0},{2,1},{3,2},{5,4},{6,5},{7,6},{9,8},{10,9},{11,10},{13,12},{... | collective-permute-start | bytes 245768 | tf_op jit(solution)/shard_map/ppermute | solution.py:20
  35.8 33.0 %copy-start = (f32[2,32]{1,0:T(2,128)S(1)}, f32[2,32]{1,0:T(2,128)}, u32[]{:S(2)}) copy-start(f32[2,32]{1,0:T(2,128)} %param.16) | copy-start | bytes 772
  69.7 6.7 %collective-permute-start.4 = (bf16[32,4,1,128]{3,2,1,0:T(2,128)(2,1)S(1)}, bf16[32,4,1,128]{3,2,1,0:T(2,128)(2,1)S(1)}, u32[]{:S(2)}, u32[]{:S(2)}) collective-permute-start(bf16[32,4,1,128]{3,2,1,0:T(2,128)(2,1)S(1)} %get-tuple-element.59), channel_id=1, source_target_pairs={{0,4},{4,8},{8,12},{1,5},{5,9},{9,13},{2,6},{6,10},{10,14},{3,7},{... | collective-permute-start | bytes 98312 | tf_op jit(solution)/shard_map/ppermute | solution.py:18
  71.0 6.7 %collective-permute-start.5 = (bf16[32,4,1,128]{3,2,1,0:T(2,128)(2,1)S(1)}, bf16[32,4,1,128]{3,2,1,0:T(2,128)(2,1)S(1)}, u32[]{:S(2)}, u32[]{:S(2)}) collective-permute-start(bf16[32,4,1,128]{3,2,1,0:T(2,128)(2,1)S(1)} %get-tuple-element.60), channel_id=1, source_target_pairs={{4,0},{8,4},{12,8},{5,1},{9,5},{13,9},{6,2},{10,6},{14,10},{7,3},{... | collective-permute-start | bytes 98312 | tf_op jit(solution)/shard_map/ppermute | solution.py:20
  77.8 5.1 %collective-permute-start.6 = (bf16[32,1,10,128]{3,2,1,0:T(8,128)(2,1)S(1)}, bf16[32,1,10,128]{3,2,1,0:T(8,128)(2,1)S(1)}, u32[]{:S(2)}, u32[]{:S(2)}) collective-permute-start(bf16[32,1,10,128]{3,2,1,0:T(8,128)(2,1)S(1)} %get-tuple-element.53), channel_id=1, source_target_pairs={{0,1},{1,2},{2,3},{4,5},{5,6},{6,7},{8,9},{9,10},{10,11},{12,13},{... | collective-permute-start | bytes 245768 | tf_op jit(solution)/shard_map/ppermute | solution.py:18
  80.4 6.9 %collective-permute-start.7 = (bf16[32,1,10,128]{3,2,1,0:T(8,128)(2,1)S(1)}, bf16[32,1,10,128]{3,2,1,0:T(8,128)(2,1)S(1)}, u32[]{:S(2)}, u32[]{:S(2)}) collective-permute-start(bf16[32,1,10,128]{3,2,1,0:T(8,128)(2,1)S(1)} %get-tuple-element.54), channel_id=1, source_target_pairs={{1,0},{2,1},{3,2},{5,4},{6,5},{7,6},{9,8},{10,9},{11,10},{13,12},{... | collective-permute-start | bytes 245768 | tf_op jit(solution)/shard_map/ppermute | solution.py:20
  140.0 8.0 %collective-permute-start.9 = (bf16[32,1,1024]{2,0,1:T(8,128)(2,1)S(1)}, bf16[32,1,1024]{2,0,1:T(8,128)(2,1)S(1)}, u32[]{:S(2)}, u32[]{:S(2)}) collective-permute-start(bf16[32,1,1024]{2,0,1:T(8,128)(2,1)S(1)} %get-tuple-element.81), channel_id=1, source_target_pairs={{1,0},{2,1},{3,2},{5,4},{6,5},{7,6},{9,8},{10,9},{11,10},{13,12},{... | collective-permute-start | bytes 196616 | tf_op jit(solution)/shard_map/ppermute | solution.py:20
  141.3 6.7 %collective-permute-start.8 = (bf16[32,1,1024]{2,0,1:T(8,128)(2,1)S(1)}, bf16[32,1,1024]{2,0,1:T(8,128)(2,1)S(1)}, u32[]{:S(2)}, u32[]{:S(2)}) collective-permute-start(bf16[32,1,1024]{2,0,1:T(8,128)(2,1)S(1)} %get-tuple-element.82), channel_id=1, source_target_pairs={{0,1},{1,2},{2,3},{4,5},{5,6},{6,7},{8,9},{9,10},{10,11},{12,13},{... | collective-permute-start | bytes 196616 | tf_op jit(solution)/shard_map/ppermute | solution.py:18
  149.9 13.3 %copy-start.1 = (f32[2,16]{1,0:T(2,128)S(1)}, f32[2,16]{1,0:T(2,128)}, u32[]{:S(2)}) copy-start(f32[2,16]{1,0:T(2,128)} %param.18) | copy-start | bytes 388
  164.9 48.3 %collective-permute-start.10 = (bf16[16,1,1024]{2,1,0:T(2,128)(2,1)S(1)}, bf16[16,1,1024]{2,1,0:T(2,128)(2,1)S(1)}, u32[]{:S(2)}, u32[]{:S(2)}) collective-permute-start(bf16[16,1,1024]{2,1,0:T(2,128)(2,1)S(1)} %get-tuple-element.101), channel_id=1, source_target_pairs={{0,1},{1,2},{2,3},{4,5},{5,6},{6,7},{8,9},{9,10},{10,11},{12,13},{... | collective-permute-start | bytes 98312 | tf_op jit(solution)/shard_map/ppermute | solution.py:18
  166.9 46.3 %collective-permute-start.11 = (bf16[16,1,1024]{2,1,0:T(2,128)(2,1)S(1)}, bf16[16,1,1024]{2,1,0:T(2,128)(2,1)S(1)}, u32[]{:S(2)}, u32[]{:S(2)}) collective-permute-start(bf16[16,1,1024]{2,1,0:T(2,128)(2,1)S(1)} %get-tuple-element.102), channel_id=1, source_target_pairs={{1,0},{2,1},{3,2},{5,4},{6,5},{7,6},{9,8},{10,9},{11,10},{13,12},{... | collective-permute-start | bytes 98312 | tf_op jit(solution)/shard_map/ppermute | solution.py:20
where the time goes:
time: 250 us; the launch traced here: 249 us
  blocking collectives  142 us (57%)
  local copies, waits for them, and re-layouts  27.2 us (11%)
  other arithmetic  26.6 us (11%)
  starting transfers between devices  25.3 us (10%)
  waiting for transfers between devices  12.9 us (5%)
  matrix products  11.3 us (5%)
  between operations  3.99 us (2%)
    psum x2, blocking collectives, fine_stats(): lax.psum((jnp.sum(flat_rows, axis=1), jnp.sum(flat_rows * flat_rows, axis...  61.8 us
    pmax x1, blocking collectives, per_device(): peaks = lax.pmax(peaks, ('sample', 'sy', 'sz'))  41.5 us
    psum x2, blocking collectives, coarse_stats(): lax.psum((jnp.sum(flat_rows, axis=1), jnp.sum(flat_rows * flat_rows, axis...  21.6 us
    ppermute x6, starting transfers between devices, padded_2(): lax.ppermute(tail, axis, [(i, (i + 1) % count) for i in range(ends)])  17.4 us
    ppermute x6, waiting for transfers between devices, padded_2(): lax.ppermute(head, axis, [((i + 1) % count, i) for i in range(ends)])  10.2 us
    all_gather x1, blocking collectives, per_device(): lax.all_gather(limited(pooled, bounds[2]), 'sy', axis=2, tiled=True)  8.94 us
    all_gather x1, blocking collectives, per_device(): lax.all_gather(edged, 'sy', axis=0, tiled=True)  8.15 us
    slice x1, local copies, waits for them, and re-layouts, level_two_conv(): stacked[:, z_tap:z_tap + out_depth, y_tap * row_len:y_tap * row_len + fla...  8.01 us
  transfers between devices with their start and end apart: 12, of which 6 were waited for; matrix products, arithmetic and copies ran while one was open for 6% of the time, Pallas kernels for 0%

commit v1 on v0

--- a/solution.py
+++ b/solution.py
@@ -39,7 +39,7 @@
 def fine_stats(values):
     flat_rows = values.reshape(values.shape[0], -1)
     return lax.psum(
-        (jnp.sum(flat_rows, axis=1), jnp.sum(flat_rows * flat_rows, axis=1)), ("sy", "sz")
+        lax.psum((jnp.sum(flat_rows, axis=1), jnp.sum(flat_rows * flat_rows, axis=1)), "sz"), "sy"
     )
 
 

time: 250 us -> 219 us (0.88)
  blocking collectives: 142 us -> 111 us
    psum x2, blocking collectives: 61.8 us -> 18.3 us  [fine_stats(): lax.psum((jnp.sum(flat_rows, axis=1), jnp.sum(flat_rows * flat_rows, axis...]
    psum x0 -> x2, blocking collectives: none -> 15.1 us  [fine_stats(): lax.psum(lax.psum((jnp.sum(flat_rows, axis=1), jnp.sum(flat_rows * flat_r...]
  transfers between devices with their start and end apart: 12 -> 12, of which waited for: 6 -> 5; matrix products, arithmetic and copies ran while one was open for 6% -> 7% of each run, Pallas kernels for 0% -> 0%
where the time goes in v1:
time: 219 us; the launch traced here: 218 us
  blocking collectives  111 us (51%)
  local copies, waits for them, and re-layouts  27.2 us (12%)
  other arithmetic  26.6 us (12%)
  starting transfers between devices  26 us (12%)
  waiting for transfers between devices  11.7 us (5%)
  matrix products  11.3 us (5%)
  between operations  4 us (2%)
    pmax x1, blocking collectives, per_device(): peaks = lax.pmax(peaks, ('sample', 'sy', 'sz'))  41.5 us
    psum x2, blocking collectives, coarse_stats(): lax.psum((jnp.sum(flat_rows, axis=1), jnp.sum(flat_rows * flat_rows, axis...  21.6 us
    psum x2, blocking collectives, fine_stats(): lax.psum((jnp.sum(flat_rows, axis=1), jnp.sum(flat_rows * flat_rows, axis...  18.3 us
    ppermute x6, starting transfers between devices, padded_2(): lax.ppermute(tail, axis, [(i, (i + 1) % count) for i in range(ends)])  18 us
    psum x2, blocking collectives, fine_stats(): lax.psum(lax.psum((jnp.sum(flat_rows, axis=1), jnp.sum(flat_rows * flat_r...  15.1 us
    ppermute x6, waiting for transfers between devices, padded_2(): lax.ppermute(head, axis, [((i + 1) % count, i) for i in range(ends)])  9 us
    all_gather x1, blocking collectives, per_device(): lax.all_gather(edged, 'sy', axis=0, tiled=True)  8.15 us
    slice x1, local copies, waits for them, and re-layouts, level_two_conv(): stacked[:, z_tap:z_tap + out_depth, y_tap * row_len:y_tap * row_len + fla...  8.01 us
  transfers between devices with their start and end apart: 12, of which 5 were waited for; matrix products, arithmetic and copies ran while one was open for 7% of the time, Pallas kernels for 0%

profile of v1, /device:TPU:0, one launch (start us, length us, event | category | flops | bytes accessed | tf_op | source)
XLA Modules:
  0.0 217.9 jit_solution(7758528016216269371)
XLA Ops:
  4.5 2.4 %collective-permute-start = (bf16[32,4,1,128]{3,2,1,0:T(2,128)(2,1)S(1)}, bf16[32,4,1,128]{3,2,1,0:T(2,128)(2,1)S(1)}, u32[]{:S(2)}, u32[]{:S(2)}) collective-permute-start(bf16[32,4,1,128]{3,2,1,0:T(2,128)(2,1)S(1)} %get-tuple-element.65), channel_id=1, source_target_pairs={{0,4},{4,8},{8,12},{1,5},{5,9},{9,13},{2,6},{6,10},{10,14},{3,7},{... | collective-permute-start | bytes 98312 | tf_op jit(solution)/shard_map/ppermute | solution.py:18
  13.2 1.7 fusion.57
  16.6 4.3 %collective-permute-start.2 = (bf16[32,1,10,128]{3,2,1,0:T(8,128)(2,1)S(1)}, bf16[32,1,10,128]{3,2,1,0:T(8,128)(2,1)S(1)}, u32[]{:S(2)}, u32[]{:S(2)}) collective-permute-start(bf16[32,1,10,128]{3,2,1,0:T(8,128)(2,1)S(1)} %get-tuple-element.59), channel_id=1, source_target_pairs={{0,1},{1,2},{2,3},{4,5},{5,6},{6,7},{8,9},{9,10},{10,11},{12,13},{... | collective-permute-start | bytes 245768 | tf_op jit(solution)/shard_map/ppermute | solution.py:18
  23.4 4.6 %collective-permute-done.3 = bf16[32,1,10,128]{3,2,1,0:T(8,128)(2,1)S(1)} collective-permute-done((bf16[32,1,10,128]{3,2,1,0:T(8,128)(2,1)S(1)}, bf16[32,1,10,128]{3,2,1,0:T(8,128)(2,1)S(1)}, u32[]{:S(2)}, u32[]{:S(2)}) %collective-permute-start.3) | collective-permute-done | bytes 81952 | tf_op jit(solution)/shard_map/ppermute | solution.py:20
  28.0 1.8 fusion.11
  37.0 9.9 %all-reduce.11 = (f32[32]{0:T(128)S(1)}, f32[32]{0:T(128)S(1)}) all-reduce(f32[32]{0:T(128)S(1)} %get-tuple-element.123, f32[32]{0:T(128)S(1)} %reduce_sum.72), channel_id=1, replica_groups=mesh['sample'=2,'sy'=4,'sz'=4] {'sz'}, use_global_device_ids=true, to_apply=%region_5.6 | all-reduce | flops 64 | bytes 512 | tf_op jit(solution)/shard_map/psum | solution.py:42
  47.0 7.4 %all-reduce.13 = (f32[32]{0:T(128)S(1)}, f32[32]{0:T(128)S(1)}) all-reduce(f32[32]{0:T(128)S(1)} %get-tuple-element.9, f32[32]{0:T(128)S(1)} %get-tuple-element.10), channel_id=1, replica_groups=mesh['sample'=2,'sy'=4,'sz'=4] {'sy'}, use_global_device_ids=true, to_apply=%region_6.7 | all-reduce | flops 64 | bytes 512 | tf_op jit(solution)/shard_map/psum | solution.py:41
  55.3 2.3 %collective-permute-start.4 = (bf16[32,4,1,128]{3,2,1,0:T(2,128)(2,1)S(1)}, bf16[32,4,1,128]{3,2,1,0:T(2,128)(2,1)S(1)}, u32[]{:S(2)}, u32[]{:S(2)}) collective-permute-start(bf16[32,4,1,128]{3,2,1,0:T(2,128)(2,1)S(1)} %get-tuple-element.63), channel_id=1, source_target_pairs={{0,4},{4,8},{8,12},{1,5},{5,9},{9,13},{2,6},{6,10},{10,14},{3,7},{... | collective-permute-start | bytes 98312 | tf_op jit(solution)/shard_map/ppermute | solution.py:18
  63.1 2.5 %collective-permute-start.6 = (bf16[32,1,10,128]{3,2,1,0:T(8,128)(2,1)S(1)}, bf16[32,1,10,128]{3,2,1,0:T(8,128)(2,1)S(1)}, u32[]{:S(2)}, u32[]{:S(2)}) collective-permute-start(bf16[32,1,10,128]{3,2,1,0:T(8,128)(2,1)S(1)} %get-tuple-element.57), channel_id=1, source_target_pairs={{0,1},{1,2},{2,3},{4,5},{5,6},{6,7},{8,9},{9,10},{10,11},{12,13},{... | collective-permute-start | bytes 245768 | tf_op jit(solution)/shard_map/ppermute | solution.py:18
  68.1 4.4 %collective-permute-done.7 = bf16[32,1,10,128]{3,2,1,0:T(8,128)(2,1)S(1)} collective-permute-done((bf16[32,1,10,128]{3,2,1,0:T(8,128)(2,1)S(1)}, bf16[32,1,10,128]{3,2,1,0:T(8,128)(2,1)S(1)}, u32[]{:S(2)}, u32[]{:S(2)}) %collective-permute-start.7) | collective-permute-done | bytes 81952 | tf_op jit(solution)/shard_map/ppermute | solution.py:20
  72.5 1.8 select_maximum_fusion
  82.1 8.4 %all-reduce.10 = (f32[32]{0:T(128)S(1)}, f32[32]{0:T(128)S(1)}) all-reduce(f32[32]{0:T(128)S(1)} %get-tuple-element.125, f32[32]{0:T(128)S(1)} %reduce_sum.74), channel_id=1, replica_groups=mesh['sample'=2,'sy'=4,'sz'=4] {'sz'}, use_global_device_ids=true, to_apply=%region_11.12 | all-reduce | flops 64 | bytes 512 | tf_op jit(solution)/shard_map/psum | solution.py:42
  90.5 7.7 %all-reduce.12 = (f32[32]{0:T(128)S(1)}, f32[32]{0:T(128)S(1)}) all-reduce(f32[32]{0:T(128)S(1)} %get-tuple-element.7, f32[32]{0:T(128)S(1)} %get-tuple-element.8), channel_id=1, replica_groups=mesh['sample'=2,'sy'=4,'sz'=4] {'sy'}, use_global_device_ids=true, to_apply=%region_12.13 | all-reduce | flops 64 | bytes 512 | tf_op jit(solution)/shard_map/psum | solution.py:41
  98.2 2.9 %fusion.16 = bf16[32,2,4,64]{0,3,2,1:T(8,128)(2,1)S(1)} fusion(f32[32]{0:T(128)S(1)} %get-tuple-element.109, f32[32]{0:T(128)S(1)} %get-tuple-element.120, f32[32,2,2,4,2,64,2]{0,6,5,4,3,2,1:T(2,128)S(1)} %bitcast.322, f32[32]{0:T(128)S(1)} %get-tuple-element.119), kind=kLoop, calls=%fused_computation.59 | loop fusion | flops 1032192 | bytes 557440 | tf_op jit(solution)/shard_map/reduce_max | solution.py:152
  102.0 6.5 %all_gather.6 = bf16[32,2,16,64]{3,0,1,2:T(8,128)(2,1)S(1)} all-gather(bf16[32,2,4,64]{3,0,1,2:T(8,128)(2,1)S(1)} %copy.195), channel_id=1, replica_groups=mesh['sample'=2,'sy'=4,'sz'=4] {'sy'}, dimensions={2}, use_global_device_ids=true | all-gather | bytes 163840 | tf_op jit(solution)/shard_map/all_gather | solution.py:154
  110.1 4.5 %collective-permute-start.8 = (bf16[32,1,1024]{2,0,1:T(8,128)(2,1)S(1)}, bf16[32,1,1024]{2,0,1:T(8,128)(2,1)S(1)}, u32[]{:S(2)}, u32[]{:S(2)}) collective-permute-start(bf16[32,1,1024]{2,0,1:T(8,128)(2,1)S(1)} %get-tuple-element.86), channel_id=1, source_target_pairs={{0,1},{1,2},{2,3},{4,5},{5,6},{6,7},{8,9},{9,10},{10,11},{12,13},{... | collective-permute-start | bytes 196616 | tf_op jit(solution)/shard_map/ppermute | solution.py:18
  120.1 11.7 %all-reduce.9 = (f32[16]{0:T(128)S(1)}, f32[16]{0:T(128)S(1)}) all-reduce(f32[16]{0:T(128)S(1)} %get-tuple-element.127, f32[16]{0:T(128)S(1)} %reduce_sum.76), channel_id=1, replica_groups=mesh['sample'=2,'sy'=4,'sz'=4] {'sz'}, use_global_device_ids=true, to_apply=%region_17.18 | all-reduce | flops 32 | bytes 256 | tf_op jit(solution)/shard_map/psum | solution.py:48
  133.5 2.0 collective-permute-start.10
  136.8 2.6 %pad_maximum_fusion.11 = f32[4]{0:T(128)S(1)} fusion(f32[1]{0:T(128)} %bitcast.57, f32[1]{0:T(128)} %bitcast.56, f32[1]{0:T(128)} %bitcast.55, f32[1]{0:T(128)} %bitcast.54), kind=kLoop, calls=%fused_computation.203 | loop fusion | flops 12 | bytes 32 | tf_op jit(solution)/shard_map/stack | solution.py:170
  140.3 41.5 %pmax.7 = f32[4]{0:T(128)} all-reduce(f32[4]{0:T(128)S(1)} %pad_maximum_fusion.11), channel_id=1, replica_groups=mesh['sample'=2,'sy'=4,'sz'=4] {'sample','sy','sz'}, use_global_device_ids=true, to_apply=%region_26.27 | all-reduce | flops 4 | bytes 32 | tf_op jit(solution)/shard_map/pmax | solution.py:172
  182.0 8.1 %all_gather.7 = bf16[64,4,1024]{2,1,0:T(4,128)(2,1)S(1)} all-gather(bf16[16,4,1024]{2,1,0:T(4,128)(2,1)S(1)} %pad_maximum_fusion.10), channel_id=1, replica_groups=mesh['sample'=2,'sy'=4,'sz'=4] {'sy'}, dimensions={0}, use_global_device_ids=true | all-gather | bytes 655360 | tf_op jit(solution)/shard_map/all_gather | solution.py:163
  191.9 3.0 %pad_maximum_fusion.2 = bf16[192,4,1152]{2,1,0:T(4,128)(2,1)S(1)} fusion(bf16[64,4,1152]{2,1,0:T(4,128)(2,1)S(1)} %pad_slice_fusion, bf16[64,4,1152]{2,1,0:T(4,128)(2,1)S(1)} %pad_slice_fusion.1, bf16[64,4,1152]{2,1,0:T(4,128)(2,1)S(1)} %pad_slice_fusion.2), kind=kLoop, calls=%fused_computation.39 | loop fusion | flops 1769472 | bytes 3538944 | tf_op jit(solution)/shard_map/concatenate | solution.py:94
  194.9 8.0 %fusion.78 = (bf16[192,2,1024]{2,1,0:T(2,128)(2,1)S(1)}, bf16[192,2,1024]{2,1,0:T(2,128)(2,1)S(1)}, bf16[192,2,1024]{2,1,0:T(2,128)(2,1)S(1)}, bf16[192,2,1024]{...) fusion(bf16[192,4,1152]{2,1,0:T(4,128)(2,1)S(1)} %pad_maximum_f, ...), kind=kLoop, calls=%fused_computation.218 | loop fusion | bytes 14155776 | tf_op jit(solution)/shard_map/slice | solution.py:109
  207.1 9.9 %all-reduce.8 = (f32[16]{0:T(128)S(1)}, f32[16]{0:T(128)S(1)}) all-reduce(f32[16]{0:T(128)S(1)} %get-tuple-element.129, f32[16]{0:T(128)S(1)} %reduce_sum.78), channel_id=1, replica_groups=mesh['sample'=2,'sy'=4,'sz'=4] {'sz'}, use_global_device_ids=true, to_apply=%region_21.22 | all-reduce | flops 32 | bytes 256 | tf_op jit(solution)/shard_map/psum | solution.py:48
  (207 shorter events, 53.9 us)
Async XLA Ops:
  4.5 12.0 %collective-permute-start = (bf16[32,4,1,128]{3,2,1,0:T(2,128)(2,1)S(1)}, bf16[32,4,1,128]{3,2,1,0:T(2,128)(2,1)S(1)}, u32[]{:S(2)}, u32[]{:S(2)}) collective-permute-start(bf16[32,4,1,128]{3,2,1,0:T(2,128)(2,1)S(1)} %get-tuple-element.65), channel_id=1, source_target_pairs={{0,4},{4,8},{8,12},{1,5},{5,9},{9,13},{2,6},{6,10},{10,14},{3,7},{... | collective-permute-start | bytes 98312 | tf_op jit(solution)/shard_map/ppermute | solution.py:18
  6.9 9.6 %collective-permute-start.1 = (bf16[32,4,1,128]{3,2,1,0:T(2,128)(2,1)S(1)}, bf16[32,4,1,128]{3,2,1,0:T(2,128)(2,1)S(1)}, u32[]{:S(2)}, u32[]{:S(2)}) collective-permute-start(bf16[32,4,1,128]{3,2,1,0:T(2,128)(2,1)S(1)} %get-tuple-element.66), channel_id=1, source_target_pairs={{4,0},{8,4},{12,8},{5,1},{9,5},{13,9},{6,2},{10,6},{14,10},{7,3},{... | collective-permute-start | bytes 98312 | tf_op jit(solution)/shard_map/ppermute | solution.py:20
  16.6 6.8 %collective-permute-start.2 = (bf16[32,1,10,128]{3,2,1,0:T(8,128)(2,1)S(1)}, bf16[32,1,10,128]{3,2,1,0:T(8,128)(2,1)S(1)}, u32[]{:S(2)}, u32[]{:S(2)}) collective-permute-start(bf16[32,1,10,128]{3,2,1,0:T(8,128)(2,1)S(1)} %get-tuple-element.59), channel_id=1, source_target_pairs={{0,1},{1,2},{2,3},{4,5},{5,6},{6,7},{8,9},{9,10},{10,11},{12,13},{... | collective-permute-start | bytes 245768 | tf_op jit(solution)/shard_map/ppermute | solution.py:18
  20.9 7.1 %collective-permute-start.3 = (bf16[32,1,10,128]{3,2,1,0:T(8,128)(2,1)S(1)}, bf16[32,1,10,128]{3,2,1,0:T(8,128)(2,1)S(1)}, u32[]{:S(2)}, u32[]{:S(2)}) collective-permute-start(bf16[32,1,10,128]{3,2,1,0:T(8,128)(2,1)S(1)} %get-tuple-element.60), channel_id=1, source_target_pairs={{1,0},{2,1},{3,2},{5,4},{6,5},{7,6},{9,8},{10,9},{11,10},{13,12},{... | collective-permute-start | bytes 245768 | tf_op jit(solution)/shard_map/ppermute | solution.py:20
  35.8 18.5 %copy-start = (f32[2,32]{1,0:T(2,128)S(1)}, f32[2,32]{1,0:T(2,128)}, u32[]{:S(2)}) copy-start(f32[2,32]{1,0:T(2,128)} %param.16) | copy-start | bytes 772
  55.3 7.7 %collective-permute-start.4 = (bf16[32,4,1,128]{3,2,1,0:T(2,128)(2,1)S(1)}, bf16[32,4,1,128]{3,2,1,0:T(2,128)(2,1)S(1)}, u32[]{:S(2)}, u32[]{:S(2)}) collective-permute-start(bf16[32,4,1,128]{3,2,1,0:T(2,128)(2,1)S(1)} %get-tuple-element.63), channel_id=1, source_target_pairs={{0,4},{4,8},{8,12},{1,5},{5,9},{9,13},{2,6},{6,10},{10,14},{3,7},{... | collective-permute-start | bytes 98312 | tf_op jit(solution)/shard_map/ppermute | solution.py:18
  57.5 5.4 %collective-permute-start.5 = (bf16[32,4,1,128]{3,2,1,0:T(2,128)(2,1)S(1)}, bf16[32,4,1,128]{3,2,1,0:T(2,128)(2,1)S(1)}, u32[]{:S(2)}, u32[]{:S(2)}) collective-permute-start(bf16[32,4,1,128]{3,2,1,0:T(2,128)(2,1)S(1)} %get-tuple-element.64), channel_id=1, source_target_pairs={{4,0},{8,4},{12,8},{5,1},{9,5},{13,9},{6,2},{10,6},{14,10},{7,3},{... | collective-permute-start | bytes 98312 | tf_op jit(solution)/shard_map/ppermute | solution.py:20
  63.1 5.0 %collective-permute-start.6 = (bf16[32,1,10,128]{3,2,1,0:T(8,128)(2,1)S(1)}, bf16[32,1,10,128]{3,2,1,0:T(8,128)(2,1)S(1)}, u32[]{:S(2)}, u32[]{:S(2)}) collective-permute-start(bf16[32,1,10,128]{3,2,1,0:T(8,128)(2,1)S(1)} %get-tuple-element.57), channel_id=1, source_target_pairs={{0,1},{1,2},{2,3},{4,5},{5,6},{6,7},{8,9},{9,10},{10,11},{12,13},{... | collective-permute-start | bytes 245768 | tf_op jit(solution)/shard_map/ppermute | solution.py:18
  65.6 6.9 %collective-permute-start.7 = (bf16[32,1,10,128]{3,2,1,0:T(8,128)(2,1)S(1)}, bf16[32,1,10,128]{3,2,1,0:T(8,128)(2,1)S(1)}, u32[]{:S(2)}, u32[]{:S(2)}) collective-permute-start(bf16[32,1,10,128]{3,2,1,0:T(8,128)(2,1)S(1)} %get-tuple-element.58), channel_id=1, source_target_pairs={{1,0},{2,1},{3,2},{5,4},{6,5},{7,6},{9,8},{10,9},{11,10},{13,12},{... | collective-permute-start | bytes 245768 | tf_op jit(solution)/shard_map/ppermute | solution.py:20
  108.8 7.8 %collective-permute-start.9 = (bf16[32,1,1024]{2,0,1:T(8,128)(2,1)S(1)}, bf16[32,1,1024]{2,0,1:T(8,128)(2,1)S(1)}, u32[]{:S(2)}, u32[]{:S(2)}) collective-permute-start(bf16[32,1,1024]{2,0,1:T(8,128)(2,1)S(1)} %get-tuple-element.85), channel_id=1, source_target_pairs={{1,0},{2,1},{3,2},{5,4},{6,5},{7,6},{9,8},{10,9},{11,10},{13,12},{... | collective-permute-start | bytes 196616 | tf_op jit(solution)/shard_map/ppermute | solution.py:20
  110.1 6.4 %collective-permute-start.8 = (bf16[32,1,1024]{2,0,1:T(8,128)(2,1)S(1)}, bf16[32,1,1024]{2,0,1:T(8,128)(2,1)S(1)}, u32[]{:S(2)}, u32[]{:S(2)}) collective-permute-start(bf16[32,1,1024]{2,0,1:T(8,128)(2,1)S(1)} %get-tuple-element.86), channel_id=1, source_target_pairs={{0,1},{1,2},{2,3},{4,5},{5,6},{6,7},{8,9},{9,10},{10,11},{12,13},{... | collective-permute-start | bytes 196616 | tf_op jit(solution)/shard_map/ppermute | solution.py:18
  118.5 13.3 %copy-start.1 = (f32[2,16]{1,0:T(2,128)S(1)}, f32[2,16]{1,0:T(2,128)}, u32[]{:S(2)}) copy-start(f32[2,16]{1,0:T(2,128)} %param.18) | copy-start | bytes 388
  133.5 48.3 %collective-permute-start.10 = (bf16[16,1,1024]{2,1,0:T(2,128)(2,1)S(1)}, bf16[16,1,1024]{2,1,0:T(2,128)(2,1)S(1)}, u32[]{:S(2)}, u32[]{:S(2)}) collective-permute-start(bf16[16,1,1024]{2,1,0:T(2,128)(2,1)S(1)} %get-tuple-element.105), channel_id=1, source_target_pairs={{0,1},{1,2},{2,3},{4,5},{5,6},{6,7},{8,9},{9,10},{10,11},{12,13},{... | collective-permute-start | bytes 98312 | tf_op jit(solution)/shard_map/ppermute | solution.py:18
  135.5 46.3 %collective-permute-start.11 = (bf16[16,1,1024]{2,1,0:T(2,128)(2,1)S(1)}, bf16[16,1,1024]{2,1,0:T(2,128)(2,1)S(1)}, u32[]{:S(2)}, u32[]{:S(2)}) collective-permute-start(bf16[16,1,1024]{2,1,0:T(2,128)(2,1)S(1)} %get-tuple-element.106), channel_id=1, source_target_pairs={{1,0},{2,1},{3,2},{5,4},{6,5},{7,6},{9,8},{10,9},{11,10},{13,12},{... | collective-permute-start | bytes 98312 | tf_op jit(solution)/shard_map/ppermute | solution.py:20
